TPU v7x, 32 devices: a whole 2x2x4 slice. The times are simulated.
32 devices in a mesh: dp: 16 (over z, x, core), tensor: 2 (over y).
Axes of the slice: x: 2, y: 2, z: 4, core: 2. Of those that a mesh axis runs over, the one named last changes fastest.
Arguments:
- hidden_in: bfloat16 [4096, 1152], P('dp'), may hold values from -6 to 6
- condition: bfloat16 [112, 1152], P('dp'), may hold values from -6 to 6
- heights: int32 [16, 7], P('dp'), may hold values from 3 to 6, as said below
- widths: int32 [16, 7], P('dp'), may hold values from 3 to 6, as said below
- ada_weight: bfloat16 [1152, 6912], P('dp', 'tensor'), may hold values from -0.1875 to 0.1875
- attn_weight: bfloat16 [1152, 4, 1152], P('dp', None, 'tensor'), may hold values from -0.1875 to 0.1875
- forget_weight: bfloat16 [1152, 16], P('dp', 'tensor'), may hold values from -0.1875 to 0.1875
- forget_bias: float32 [16], P('tensor'), may hold values from -4 to 3
- conv_weight: bfloat16 [9, 1152], P(None, 'tensor'), may hold values from -1.796875 to 1.796875
- out_weight: bfloat16 [1152, 1152], P('tensor', 'dp'), may hold values from -0.1875 to 0.1875
- up_weight: bfloat16 [1152, 4608], P('dp', 'tensor'), may hold values from -0.1875 to 0.1875
- down_weight: bfloat16 [4608, 1152], P('tensor', 'dp'), may hold values from -0.09375 to 0.09375
- cotangent: bfloat16 [4096, 1152], P('dp'), may hold values from -6 to 6
Outputs:
- hidden_out: bfloat16 [4096, 1152], P('dp')
- grad_hidden: bfloat16 [4096, 1152], P('dp')
- grad_condition: bfloat16 [112, 1152], P('dp')
- grad_ada: float32 [1152, 6912], P('dp', 'tensor')
- grad_attn: float32 [1152, 4, 1152], P('dp', None, 'tensor')
- grad_forget: float32 [1152, 16], P('dp', 'tensor')
- grad_bias: float32 [16], P('tensor')
- grad_conv: float32 [9, 1152], P(None, 'tensor')
- grad_out_weight: float32 [1152, 1152], P('tensor', 'dp')
- grad_up: float32 [1152, 4608], P('dp', 'tensor')
- grad_down: float32 [4608, 1152], P('tensor', 'dp')
Inputs may be any that keep to these rules, and one draw needn't show every extreme that they name: `heights`: each packed sequence holds 7 images laid back to back from its first slot; the slots after them are empty. `widths`: as for heights.
All inputs are finite; a program needn't handle non-finite values.
Results may differ from a plain program's by a relative error of at most 0.011.
Values may be sent and summed in bfloat16 or wider, within the bound.
A program may use at most 256 MiB of HBM per device.

v0:
```python
import functools
import jax
import jax.numpy as jnp
from jax import lax
from jax.sharding import PartitionSpec as P

BLOCK = 64
gate_norm = 16.0
norm_epsilon = 1e-06
head_epsilon = 1e-05
highest_precision = lax.Precision.HIGHEST


def layout(heights, widths, length):
    sequence_count, number_of_images = heights.shape
    image_area = heights * widths
    image_ends = jnp.cumsum(image_area, axis=1)
    starts = image_ends - image_area
    position = jnp.arange(length, dtype=jnp.int32)
    segment = jnp.sum((position[None, :, None] >= image_ends[:, None, :]).astype(jnp.int32), axis=2)
    choose_rows = (
        segment[:, :, None] == jnp.arange(number_of_images, dtype=jnp.int32)[None, None, :]
    )
    zero_int = jnp.zeros((), jnp.int32)
    start_at = jnp.sum(jnp.where(choose_rows, starts[:, None, :], zero_int), axis=2)
    image_width = jnp.maximum(
        jnp.sum(jnp.where(choose_rows, widths[:, None, :], zero_int), axis=2), 1
    )
    image_height = jnp.sum(jnp.where(choose_rows, heights[:, None, :], zero_int), axis=2)
    offset_in = position[None, :] - start_at
    row_index = offset_in // image_width
    col_index = offset_in - row_index * image_width
    is_valid = segment < number_of_images
    seq_base = jnp.arange(sequence_count, dtype=jnp.int32)[:, None]
    token_keys = (segment + seq_base * (number_of_images + 1)).reshape(-1)
    tap_list = []
    for vertical in (-1, 0, 1):
        for lateral in (-1, 0, 1):
            inside = (
                is_valid
                & (row_index + vertical >= 0)
                & (row_index + vertical < image_height)
                & (col_index + lateral >= 0)
                & (col_index + lateral < image_width)
            )
            target = (
                jnp.clip(position[None, :] + vertical * image_width + lateral, 0, length - 1)
                + seq_base * length
            )
            tap_list.append((target.reshape(-1), inside.reshape(-1).astype(jnp.float32)))
    return (choose_rows.astype(jnp.float32), token_keys, tap_list)


def modulate(values, shift, scale):
    centre = values - jnp.mean(values, axis=1, keepdims=True)
    spread = jnp.mean(centre * centre, axis=1, keepdims=True)
    return centre * lax.rsqrt(spread + norm_epsilon) * (1.0 + scale) + shift


def gelu_tanh(values):
    return jax.nn.gelu(values, approximate=True)


def tensor_total(partial_terms):
    summed_half = lax.psum_scatter(partial_terms, "tensor", scatter_dimension=1, tiled=True)
    return lax.all_gather(summed_half, "tensor", axis=1, tiled=True)


def token_mixer(queries, keys_in, values, gate_raw, forget_raw, conv_kernel, token_keys, tap_list):
    number_of_tokens, channels = queries.shape
    head_count = forget_raw.shape[1]
    head_size = channels // head_count
    block_count = number_of_tokens // BLOCK
    log_decay = jax.nn.log_sigmoid(forget_raw) / gate_norm
    cumulative = jnp.cumsum(log_decay.reshape(block_count, BLOCK, head_count), axis=1)
    decay_rows = jnp.transpose(cumulative, (0, 2, 1))
    query_blocks = (jax.nn.elu(queries) + 1.0).reshape(block_count, BLOCK, head_count, head_size)
    key_blocks = (jax.nn.elu(keys_in) + 1.0).reshape(block_count, BLOCK, head_count, head_size)
    value_blocks = values.reshape(block_count, BLOCK, head_count, head_size)
    block_keys = token_keys.reshape(block_count, BLOCK)
    position = jnp.arange(BLOCK, dtype=jnp.int32)
    lower = position[:, None] >= position[None, :]
    same_heads = ((block_keys[:, :, None] == block_keys[:, None, :]) & lower[None, :, :])[
        :, None, :, :
    ]
    exponent = decay_rows[:, :, :, None] - decay_rows[:, :, None, :]
    decays = jnp.where(same_heads, jnp.exp(jnp.where(same_heads, exponent, 0.0)), 0.0)
    scores = jnp.einsum("bthk,bshk->bhts", query_blocks, key_blocks, precision=highest_precision)
    inside_part = jnp.einsum(
        "bhts,bshk->bthk", scores * decays, value_blocks, precision=highest_precision
    )
    last_decay = decay_rows[:, :, -1]
    last_key = block_keys[:, -1]
    member = (block_keys == last_key[:, None]).astype(jnp.float32)
    end_weight = member[:, :, None] * jnp.exp(last_decay[:, None, :] - cumulative)
    weighted = key_blocks * end_weight[:, :, :, None]
    summary = jnp.einsum("bshk,bshj->bhkj", weighted, value_blocks, precision=highest_precision)
    prior_key = jnp.concatenate([jnp.full((1,), -1, jnp.int32), last_key[:-1]])
    keep_state = (last_key == prior_key).astype(jnp.float32)
    factor = keep_state[:, None] * jnp.exp(last_decay)

    def advance(carry_state, inputs):
        scale_now, added = inputs
        return (scale_now[:, None, None] * carry_state + added, carry_state)

    initial = jnp.zeros((head_count, head_size, head_size), jnp.float32)
    final_state, start_states = lax.scan(advance, initial, (factor, summary))
    carries = (block_keys == prior_key[:, None]).astype(jnp.float32)
    lifted = query_blocks * jnp.exp(cumulative)[:, :, :, None] * carries[:, :, None, None]
    carried_part = jnp.einsum("bthk,bhkj->bthj", lifted, start_states, precision=highest_precision)
    attended = (inside_part + carried_part).reshape(number_of_tokens, head_count, head_size)
    normed = attended * lax.rsqrt(
        jnp.mean(attended * attended, axis=2, keepdims=True) + head_epsilon
    )
    gated_out = normed.reshape(number_of_tokens, channels) * jax.nn.silu(gate_raw)
    spatial = jnp.zeros_like(gated_out)
    for tap_number, (target, inside) in enumerate(tap_list):
        spatial = (
            spatial
            + conv_kernel[tap_number][None, :]
            * jnp.take(gated_out, target, axis=0)
            * inside[:, None]
        )
    return gated_out + spatial


def body(
    hidden_in,
    condition,
    heights,
    widths,
    ada_weight,
    attn_weight,
    forget_weight,
    forget_bias,
    conv_weight,
    out_weight,
    up_weight,
    down_weight,
    cotangent,
):
    sequence_count, number_of_images = heights.shape
    number_of_tokens, hidden_width = hidden_in.shape
    length = number_of_tokens // sequence_count
    half_width = conv_weight.shape[1]
    choose_rows, token_keys, tap_list = layout(heights, widths, length)
    shards = (ada_weight, attn_weight, forget_weight, out_weight, up_weight, down_weight)
    full_ada, full_attn, full_forget, full_out, full_up, full_down = (
        lax.all_gather(ada_weight, "dp", axis=0, tiled=True),
        lax.all_gather(attn_weight, "dp", axis=0, tiled=True),
        lax.all_gather(forget_weight, "dp", axis=0, tiled=True),
        lax.all_gather(out_weight, "dp", axis=1, tiled=True),
        lax.all_gather(up_weight, "dp", axis=0, tiled=True),
        lax.all_gather(down_weight, "dp", axis=1, tiled=True),
    )
    cond_float = condition.astype(jnp.float32)
    act_cond, silu_back = jax.vjp(jax.nn.silu, cond_float)
    act_low = act_cond.astype(jnp.bfloat16)
    mod_half = jnp.dot(act_low, full_ada, preferred_element_type=jnp.float32)
    modulation_vectors = lax.all_gather(mod_half, "tensor", axis=1, tiled=True)
    token_wise = jnp.einsum(
        "jyq,jqu->jyu",
        choose_rows,
        modulation_vectors.reshape(sequence_count, number_of_images, 6 * hidden_width),
        precision=highest_precision,
    ).reshape(number_of_tokens, 6 * hidden_width)
    shift_one, scale_one, gate_one, shift_two, scale_two, gate_two = jnp.split(
        token_wise, 6, axis=1
    )
    hidden_float = hidden_in.astype(jnp.float32)
    modulated_one, norm_one_back = jax.vjp(modulate, hidden_float, shift_one, scale_one)
    xm_one = modulated_one.astype(jnp.bfloat16)
    attn_flat = full_attn.reshape(hidden_width, 4 * half_width)
    projected = jnp.dot(xm_one, attn_flat, preferred_element_type=jnp.float32).reshape(
        number_of_tokens, 4, half_width
    )
    queries = projected[:, 0].astype(jnp.bfloat16)
    keys_low = projected[:, 1].astype(jnp.bfloat16)
    values = projected[:, 2].astype(jnp.bfloat16)
    gate_raw = projected[:, 3]
    forget_raw = jnp.dot(xm_one, full_forget, preferred_element_type=jnp.float32) + forget_bias
    mixer_local = functools.partial(token_mixer, token_keys=token_keys, tap_list=tap_list)
    mixed_out, mixer_back = jax.vjp(
        mixer_local,
        queries.astype(jnp.float32),
        keys_low.astype(jnp.float32),
        values.astype(jnp.float32),
        gate_raw,
        forget_raw,
        conv_weight.astype(jnp.float32),
    )
    mixed_low = mixed_out.astype(jnp.bfloat16)
    attn_out = tensor_total(jnp.dot(mixed_low, full_out, preferred_element_type=jnp.float32))
    after_attn = hidden_float + gate_one * attn_out
    modulated_two, norm_two_back = jax.vjp(modulate, after_attn, shift_two, scale_two)
    xm_two = modulated_two.astype(jnp.bfloat16)
    up_value = jnp.dot(xm_two, full_up, preferred_element_type=jnp.float32)
    act_value, gelu_back = jax.vjp(gelu_tanh, up_value)
    act_ffn = act_value.astype(jnp.bfloat16)
    down_value = tensor_total(jnp.dot(act_ffn, full_down, preferred_element_type=jnp.float32))
    hidden_out = (after_attn + gate_two * down_value).astype(jnp.bfloat16)
    full_ada, full_attn, full_forget, full_out, full_up, full_down = (
        lax.all_gather(shards[0], "dp", axis=0, tiled=True),
        lax.all_gather(shards[1], "dp", axis=0, tiled=True),
        lax.all_gather(shards[2], "dp", axis=0, tiled=True),
        lax.all_gather(shards[3], "dp", axis=1, tiled=True),
        lax.all_gather(shards[4], "dp", axis=0, tiled=True),
        lax.all_gather(shards[5], "dp", axis=1, tiled=True),
    )
    attn_flat = full_attn.reshape(hidden_width, 4 * half_width)
    upstream = cotangent.astype(jnp.float32)
    delta_down = (gate_two * upstream).astype(jnp.bfloat16)
    delta_gate_two = upstream * down_value
    delta_act = jnp.einsum("nd,fd->nf", delta_down, full_down, preferred_element_type=jnp.float32)
    local_down_grad = jnp.einsum(
        "nf,nd->fd", act_ffn, delta_down, preferred_element_type=jnp.float32
    )
    delta_up = gelu_back(delta_act)[0].astype(jnp.bfloat16)
    local_up_grad = jnp.einsum("nd,nf->df", xm_two, delta_up, preferred_element_type=jnp.float32)
    delta_xm_two = tensor_total(
        jnp.einsum("nf,df->nd", delta_up, full_up, preferred_element_type=jnp.float32)
    )
    delta_after, delta_shift_two, delta_scale_two = norm_two_back(delta_xm_two)
    delta_after = delta_after + upstream
    delta_attn = (gate_one * delta_after).astype(jnp.bfloat16)
    delta_gate_one = delta_after * attn_out
    local_out_grad = jnp.einsum(
        "nc,nd->cd", mixed_low, delta_attn, preferred_element_type=jnp.float32
    )
    delta_mixed = jnp.einsum("nd,cd->nc", delta_attn, full_out, preferred_element_type=jnp.float32)
    delta_query, delta_key, delta_value, delta_gate, delta_forget, delta_conv = mixer_back(
        delta_mixed
    )
    delta_proj = (
        jnp.stack([delta_query, delta_key, delta_value, delta_gate], axis=1)
        .astype(jnp.bfloat16)
        .reshape(number_of_tokens, 4 * half_width)
    )
    local_attn_grad = jnp.einsum(
        "nd,nc->dc", xm_one, delta_proj, preferred_element_type=jnp.float32
    ).reshape(hidden_width, 4, half_width)
    xm_one_float = xm_one.astype(jnp.float32)
    local_forget_grad = jnp.einsum(
        "nd,nh->dh", xm_one_float, delta_forget, precision=highest_precision
    )
    partial_back = jnp.einsum(
        "nc,dc->nd", delta_proj, attn_flat, preferred_element_type=jnp.float32
    ) + jnp.einsum(
        "nh,dh->nd", delta_forget, full_forget.astype(jnp.float32), precision=highest_precision
    )
    delta_xm_one = tensor_total(partial_back)
    delta_input, delta_shift_one, delta_scale_one = norm_one_back(delta_xm_one)
    grad_hidden = (delta_after + delta_input).astype(jnp.bfloat16)
    side_index = lax.axis_index("tensor")
    first_group = jnp.concatenate([delta_shift_one, delta_scale_one, delta_gate_one], axis=1)
    second_group = jnp.concatenate([delta_shift_two, delta_scale_two, delta_gate_two], axis=1)
    delta_tokens = jnp.where(side_index == 0, first_group, second_group)
    delta_mod = (
        jnp.einsum(
            "mxz,mxk->mzk",
            choose_rows,
            delta_tokens.reshape(sequence_count, length, 3 * hidden_width),
            precision=highest_precision,
        )
        .reshape(sequence_count * number_of_images, 3 * hidden_width)
        .astype(jnp.bfloat16)
    )
    local_ada_grad = jnp.einsum("id,ie->de", act_low, delta_mod, preferred_element_type=jnp.float32)
    delta_cond = lax.psum(
        jnp.einsum("ie,de->id", delta_mod, full_ada, preferred_element_type=jnp.float32), "tensor"
    )
    grad_condition = silu_back(delta_cond)[0].astype(jnp.bfloat16)
    grad_conv, grad_bias = lax.psum((delta_conv, jnp.sum(delta_forget, axis=0)), "dp")
    grad_ada, grad_attn, grad_forget, grad_out_weight, grad_up, grad_down = (
        lax.psum_scatter(local_ada_grad, "dp", scatter_dimension=0, tiled=True),
        lax.psum_scatter(local_attn_grad, "dp", scatter_dimension=0, tiled=True),
        lax.psum_scatter(local_forget_grad, "dp", scatter_dimension=0, tiled=True),
        lax.psum_scatter(local_out_grad, "dp", scatter_dimension=1, tiled=True),
        lax.psum_scatter(local_up_grad, "dp", scatter_dimension=0, tiled=True),
        lax.psum_scatter(local_down_grad, "dp", scatter_dimension=1, tiled=True),
    )
    return (
        hidden_out,
        grad_hidden,
        grad_condition,
        grad_ada,
        grad_attn,
        grad_forget,
        grad_bias,
        grad_conv,
        grad_out_weight,
        grad_up,
        grad_down,
    )


def solution(mesh):
    in_specs = (
        P("dp", None),
        P("dp", None),
        P("dp", None),
        P("dp", None),
        P("dp", "tensor"),
        P("dp", None, "tensor"),
        P("dp", "tensor"),
        P("tensor"),
        P(None, "tensor"),
        P("tensor", "dp"),
        P("dp", "tensor"),
        P("tensor", "dp"),
        P("dp", None),
    )
    out_specs = (
        P("dp", None),
        P("dp", None),
        P("dp", None),
        P("dp", "tensor"),
        P("dp", None, "tensor"),
        P("dp", "tensor"),
        P("tensor"),
        P(None, "tensor"),
        P("tensor", "dp"),
        P("dp", "tensor"),
        P("tensor", "dp"),
    )
    return jax.shard_map(body, mesh=mesh, in_specs=in_specs, out_specs=out_specs, check_vma=False)
```

profile of v0, /device:TPU:0, one launch (start us, length us, event | category | flops | bytes accessed | tf_op | source)
XLA Modules:
  0.0 1326.6 jit_solution(6717316120422794878)
XLA Ops:
  13.2 23.5 %all-gather = bf16[16,72,8]{1,2,0:T(8,128)(2,1)S(1)} all-gather(bf16[1,72,8]{1,2,0:T(8,128)(2,1)S(1)} %bitcast.201), channel_id=1, replica_groups=mesh['dp'=16,'tensor'=2] {'dp'}, dimensions={0}, use_global_device_ids=true | all-gather | bytes 19584 | tf_op jit(solution)/shard_map/all_gather | solution.py:151
  45.3 27.8 %all-gather.13.cloned.1.call-done = bf16[1152,4,576]{2,0,1:T(8,128)(2,1)} async-done(((bf16[72,4,576]{2,0,1:T(8,128)(2,1)}), bf16[1152,4,576]{2,0,1:T(8,128)(2,1)}) %all-gather.13.cloned.1.call-update) | async-done | bytes 5308432 | tf_op jit(solution)/shard_map/all_gather | solution.py:150
  73.1 8.5 copy.425
  81.7 63.8 %all-gather.11.cloned.1.call-done = bf16[1152,3456]{1,0:T(8,128)(2,1)} async-done(((bf16[72,3456]{1,0:T(8,128)(2,1)}), bf16[1152,3456]{1,0:T(8,128)(2,1)}) %all-gather.11.cloned.1.call-update) | async-done | bytes 7962640 | tf_op jit(solution)/shard_map/all_gather | solution.py:149
  175.7 6.6 while.34
  239.7 20.6 %reduce-scatter.29.cloned.1.call-done = f32[576,256]{1,0:T(8,128)} async-done(((f32[1152,256]{1,0:T(8,128)}), f32[576,256]{1,0:T(8,128)}) %reduce-scatter.29.cloned.1.call-update) | async-done | bytes 589840
  262.2 22.3 %all-gather.17.cloned.1.call-done = f32[256,1152]{0,1:T(8,128)} async-done(((f32[256,576]{0,1:T(8,128)}), f32[256,1152]{0,1:T(8,128)}) %all-gather.17.cloned.1.call-update) | async-done | bytes 1179664 | tf_op jit(solution)/shard_map/all_gather | solution.py:66
  292.1 50.8 %all-gather.19.cloned.1.call-done = bf16[1152,2304]{1,0:T(8,128)(2,1)} async-done(((bf16[72,2304]{1,0:T(8,128)(2,1)}), bf16[1152,2304]{1,0:T(8,128)(2,1)}) %all-gather.19.cloned.1.call-update) | async-done | bytes 5308432 | tf_op jit(solution)/shard_map/all_gather | solution.py:153
  348.7 51.3 %all-gather.21.cloned.1.call-done = bf16[2304,1152]{0,1:T(8,128)(2,1)} async-done(((bf16[2304,72]{0,1:T(8,128)(2,1)}), bf16[2304,1152]{0,1:T(8,128)(2,1)}) %all-gather.21.cloned.1.call-update) | async-done | bytes 5308432 | tf_op jit(solution)/shard_map/all_gather | solution.py:154
  416.1 14.5 %reduce-scatter.33.cloned.1.call-done = f32[576,256]{1,0:T(8,128)} async-done(((f32[1152,256]{1,0:T(8,128)}), f32[576,256]{1,0:T(8,128)}) %reduce-scatter.33.cloned.1.call-update) | async-done | bytes 589840
  430.7 24.0 %reduce-scatter.31.cloned.1.call-done = f32[576,256]{1,0:T(8,128)} async-done(((f32[1152,256]{1,0:T(8,128)}), f32[576,256]{1,0:T(8,128)}) %reduce-scatter.31.cloned.1.call-update) | async-done | bytes 589840
  455.0 23.9 %all-gather.25.cloned.1.call-done = f32[256,1152]{0,1:T(8,128)} async-done(((f32[256,576]{0,1:T(8,128)}), f32[256,1152]{0,1:T(8,128)}) %all-gather.25.cloned.1.call-update) | async-done | bytes 1179664 | tf_op jit(solution)/shard_map/all_gather | solution.py:66
  483.5 19.7 %all-gather.23.cloned.1.call-done = f32[256,1152]{0,1:T(8,128)} async-done(((f32[256,576]{0,1:T(8,128)}), f32[256,1152]{0,1:T(8,128)}) %all-gather.23.cloned.1.call-update) | async-done | bytes 1179664 | tf_op jit(solution)/shard_map/all_gather | solution.py:66
  590.5 10.2 while.35
  646.3 21.9 %reduce-scatter.35.cloned.1.call-done = f32[576,256]{1,0:T(8,128)} async-done(((f32[1152,256]{1,0:T(8,128)}), f32[576,256]{1,0:T(8,128)}) %reduce-scatter.35.cloned.1.call-update) | async-done | bytes 589840
  686.0 7.6 fusion.137
  702.8 10.0 fusion.133
  717.7 67.2 %all-reduce.13 = (f32[1152,8]{0,1:T(8,128)S(1)}, f32[8]{0:T(128)}, f32[9,576]{1,0:T(8,128)}) all-reduce(f32[1152,8]{0,1:T(8,128)S(1)} %fusion.120, f32[8]{0:T(128)S(1)} %neg.58, f32[9,576]{1,0:T(8,128)S(1)} %pad_add_fusion), channel_id=8, replica_groups=mesh['dp'=16,'tensor'=2] {'dp'}, use_global_device_ids=true, to_apply=%region_43.45.clone | all-reduce | flops 14408 | bytes 115264
  791.0 7.7 psum.21
  799.3 28.3 %reduce-scatter.23.cloned.1.call-done = f32[72,4,576]{2,0,1:T(8,128)} async-done(((f32[1152,4,576]{2,0,1:T(8,128)}), f32[72,4,576]{2,0,1:T(8,128)}) %reduce-scatter.23.cloned.1.call-update) | async-done | bytes 663568 | tf_op jit(solution)/shard_map/reduce_scatter | solution.py:276
  829.9 65.6 %reduce-scatter.39.cloned.1.call-done = f32[576,72]{0,1:T(8,128)} async-done(((f32[576,1152]{0,1:T(8,128)}), f32[576,72]{0,1:T(8,128)}) %reduce-scatter.39.cloned.1.call-update) | async-done | bytes 165904
  895.5 124.2 %reduce-scatter.25.cloned.1.call-done = f32[72,2304]{1,0:T(8,128)} async-done(((f32[1152,2304]{1,0:T(8,128)}), f32[72,2304]{1,0:T(8,128)}) %reduce-scatter.25.cloned.1.call-update) | async-done | bytes 663568 | tf_op jit(solution)/shard_map/reduce_scatter | solution.py:279
  1019.7 124.8 %reduce-scatter.27.cloned.1.call-done = f32[2304,72]{0,1:T(8,128)} async-done(((f32[2304,1152]{0,1:T(8,128)}), f32[2304,72]{0,1:T(8,128)}) %reduce-scatter.27.cloned.1.call-update) | async-done | bytes 663568 | tf_op jit(solution)/shard_map/reduce_scatter | solution.py:280
  1144.5 174.8 %reduce-scatter.37.cloned.1.call-done = f32[72,3456]{1,0:T(8,128)} async-done(((f32[1152,3456]{1,0:T(8,128)}), f32[72,3456]{1,0:T(8,128)}) %reduce-scatter.37.cloned.1.call-update) | async-done | bytes 995344
  (557 shorter events, 325.7 us)
Async XLA Ops:
  7.2 65.8 %all-gather.13.cloned.1.call-start = ((), (), s32[]{:S(2)}) async-start(), calls=%async_computation.10 | async-start | bytes 6266880 | tf_op jit(solution)/shard_map/all_gather | solution.py:150
  9.1 136.4 %all-gather.11.cloned.1.call-start = ((), (), s32[]{:S(2)}) async-start(), calls=%async_computation.9 | async-start | bytes 8460288 | tf_op jit(solution)/shard_map/all_gather | solution.py:149
  9.9 226.7 %all-gather.15.cloned.1.call-start = ((), (), s32[]{:S(2)}) async-start(), calls=%async_computation.11 | async-start | bytes 1566720 | tf_op jit(solution)/shard_map/all_gather | solution.py:152
  10.6 249.8 %reduce-scatter.29.cloned.1.call-start = ((), (), s32[]{:S(2)}) async-start(), calls=%async_computation.21 | async-start | bytes 1769472
  10.9 144.8 %copy-start.71 = (s32[256]{0:T(256)}, s32[256]{0:T(256)S(1)}, u32[]{:S(2)}) copy-start(s32[256]{0:T(256)S(1)} %fusion.123) | copy-start | bytes 3076
  12.8 145.9 %copy-start.89 = (f32[256]{0:T(256)}, f32[256]{0:T(256)S(1)}, u32[]{:S(2)}) copy-start(f32[256]{0:T(256)S(1)} %broadcast_multiply_fusion.1) | copy-start | bytes 3076
  13.1 145.6 %copy-start.103 = (f32[256]{0:T(256)}, f32[256]{0:T(256)S(1)}, u32[]{:S(2)}) copy-start(f32[256]{0:T(256)S(1)} %fusion.125) | copy-start | bytes 3076
  36.7 125.2 %copy-start.61 = (bf16[1152,8]{0,1:T(8,128)(2,1)}, bf16[1152,8]{0,1:T(8,128)(2,1)S(1)}, u32[]{:S(2)}) copy-start(bf16[1152,8]{0,1:T(8,128)(2,1)S(1)} %reshape.1109) | copy-start | bytes 55300
  172.3 406.8 %copy-start.63 = (f32[4,64,8]{1,2,0:T(8,128)}, f32[4,64,8]{1,2,0:T(8,128)S(1)}, u32[]{:S(2)}) copy-start(f32[4,64,8]{1,2,0:T(8,128)S(1)} %get-tuple-element.444) | copy-start | bytes 24580
  172.3 432.6 %copy-start.65 = (f32[4,64,8]{1,2,0:T(8,128)}, f32[4,64,8]{1,2,0:T(8,128)S(1)}, u32[]{:S(2)}) copy-start(f32[4,64,8]{1,2,0:T(8,128)S(1)} %get-tuple-element.445) | copy-start | bytes 24580
  239.7 44.8 %all-gather.17.cloned.1.call-start = ((), (), s32[]{:S(2)}) async-start(), calls=%async_computation.12 | async-start | bytes 1769472 | tf_op jit(solution)/shard_map/all_gather | solution.py:66
  260.4 82.5 %all-gather.19.cloned.1.call-start = ((), (), s32[]{:S(2)}) async-start(), calls=%async_computation.13 | async-start | bytes 5640192 | tf_op jit(solution)/shard_map/all_gather | solution.py:153
  261.0 139.1 %all-gather.21.cloned.1.call-start = ((), (), s32[]{:S(2)}) async-start(), calls=%async_computation.14 | async-start | bytes 5640192 | tf_op jit(solution)/shard_map/all_gather | solution.py:154
  261.7 168.9 %reduce-scatter.33.cloned.1.call-start = ((), (), s32[]{:S(2)}) async-start(), calls=%async_computation.23 | async-start | bytes 1769472
  410.0 44.7 %reduce-scatter.31.cloned.1.call-start = ((), (), s32[]{:S(2)}) async-start(), calls=%async_computation.22 | async-start | bytes 1769472
  416.1 62.8 %all-gather.25.cloned.1.call-start = ((), (), s32[]{:S(2)}) async-start(), calls=%async_computation.16 | async-start | bytes 1769472 | tf_op jit(solution)/shard_map/all_gather | solution.py:66
  430.7 72.6 %all-gather.23.cloned.1.call-start = ((), (), s32[]{:S(2)}) async-start(), calls=%async_computation.15 | async-start | bytes 1769472 | tf_op jit(solution)/shard_map/all_gather | solution.py:66
  454.8 213.4 %reduce-scatter.35.cloned.1.call-start = ((), (), s32[]{:S(2)}) async-start(), calls=%async_computation.24 | async-start | bytes 1769472
  646.2 47.6 %all-gather.27.cloned.1.call-start = ((), (), s32[]{:S(2)}) async-start(), calls=%async_computation.17 | async-start | bytes 1769472 | tf_op jit(solution)/shard_map/all_gather | solution.py:66
  668.2 159.5 %reduce-scatter.23.cloned.1.call-start = ((), (), s32[]{:S(2)}) async-start(), calls=%async_computation.18 | async-start | bytes 12533760 | tf_op jit(solution)/shard_map/reduce_scatter | solution.py:276
  674.5 221.0 %reduce-scatter.39.cloned.1.call-start = ((), (), s32[]{:S(2)}) async-start(), calls=%async_computation.26 | async-start | bytes 3133440
  677.9 341.8 %reduce-scatter.25.cloned.1.call-start = ((), (), s32[]{:S(2)}) async-start(), calls=%async_computation.19 | async-start | bytes 11280384 | tf_op jit(solution)/shard_map/reduce_scatter | solution.py:279
  685.0 459.5 %reduce-scatter.27.cloned.1.call-start = ((), (), s32[]{:S(2)}) async-start(), calls=%async_computation.20 | async-start | bytes 11280384 | tf_op jit(solution)/shard_map/reduce_scatter | solution.py:280
  693.7 625.6 %reduce-scatter.37.cloned.1.call-start = ((), (), s32[]{:S(2)}) async-start(), calls=%async_computation.25 | async-start | bytes 16920576
  (139 other events, 1033.5 us)
Sparse Core Ops, SparseCore 0:
  10.8 62.2 all-gather.12
  75.2 70.2 all-gather.10
  147.6 37.8 all-gather.14
  239.8 20.4 reduce-scatter.28
  261.7 22.7 all-gather.16
  286.6 56.2 all-gather.18
  345.1 54.9 all-gather.20
  410.2 20.4 reduce-scatter.32
  432.9 21.8 reduce-scatter.30
  456.1 22.7 all-gather.24
  480.5 22.7 all-gather.22
  646.3 21.8 reduce-scatter.34
  669.7 22.7 all-gather.26
  696.5 131.1 reduce-scatter.22
  832.0 63.3 reduce-scatter.38
  900.0 119.7 reduce-scatter.24
  1024.2 120.2 reduce-scatter.26
  1149.1 170.1 reduce-scatter.36
where the time goes:
time: 1340 us; the launch traced here: 1330 us
  waiting for transfers between devices  862 us (64%)
  local copies, waits for them, and re-layouts  123 us (9%)
  matrix products  123 us (9%)
  blocking collectives  104 us (8%)
  other arithmetic  95.5 us (7%)
  between operations  17.5 us (1%)
    unnamed x24, waiting for transfers between devices  324 us
    reduce_scatter x1, waiting for transfers between devices, body(): lax.psum_scatter(local_down_grad, 'dp', scatter_dimension=1, tiled=True)  125 us
    reduce_scatter x1, waiting for transfers between devices, body(): lax.psum_scatter(local_up_grad, 'dp', scatter_dimension=0, tiled=True)  124 us
    unnamed x1, blocking collectives  67.2 us
    all_gather x4, waiting for transfers between devices, tensor_total(): return lax.all_gather(summed_half, 'tensor', axis=1, tiled=True)  66 us
    all_gather x1, waiting for transfers between devices, body(): lax.all_gather(ada_weight, 'dp', axis=0, tiled=True)  63.8 us
    all_gather x1, waiting for transfers between devices, body(): lax.all_gather(down_weight, 'dp', axis=1, tiled=True)  51.3 us
    all_gather x1, waiting for transfers between devices, body(): lax.all_gather(up_weight, 'dp', axis=0, tiled=True)  50.8 us
  transfers between devices with their start and end apart: 18, of which 16 were waited for; matrix products, arithmetic and copies ran while one was open for 13% of the time, Pallas kernels for 0%

commit v1 on v0

--- a/solution.py
+++ b/solution.py
@@ -9,6 +9,28 @@
 norm_epsilon = 1e-06
 head_epsilon = 1e-05
 highest_precision = lax.Precision.HIGHEST
+
+
+def joined_along(blocks, dim):
+    dims = list(blocks.shape[1:])
+    dims[dim] *= blocks.shape[0]
+    return jnp.moveaxis(blocks, 0, dim).reshape(dims)
+
+
+def gather_around(array, axis, dim):
+    size = lax.axis_size(axis)
+    pairs = [(i, (i + 1) % size) for i in range(size)]
+    back = [(b, a) for a, b in pairs]
+    lower, upper = ([], [])
+    for hop in range(size - 1):
+        if hop % 2 == 0:
+            lower.append(lax.ppermute(lower[-1] if lower else array, axis, pairs))
+        else:
+            upper.append(lax.ppermute(upper[-1] if upper else array, axis, back))
+    parts = jnp.stack([*lower[::-1], array, *upper])
+    shift = lax.axis_index(axis) - len(lower)
+    parts = parts[(jnp.arange(size) - shift) % size]
+    return joined_along(parts, dim)
 
 
 def layout(heights, widths, length):
@@ -150,7 +172,7 @@
         lax.all_gather(attn_weight, "dp", axis=0, tiled=True),
         lax.all_gather(forget_weight, "dp", axis=0, tiled=True),
         lax.all_gather(out_weight, "dp", axis=1, tiled=True),
-        lax.all_gather(up_weight, "dp", axis=0, tiled=True),
+        gather_around(up_weight, "dp", 0),
         lax.all_gather(down_weight, "dp", axis=1, tiled=True),
     )
     cond_float = condition.astype(jnp.float32)

time: 1340 us -> 1350 us (level)
  waiting for transfers between devices: 862 us -> 822 us
  starting transfers between devices: 1.61 us -> 33.4 us
  local copies, waits for them, and re-layouts: 123 us -> 146 us
    ppermute x0 -> x15, waiting for transfers between devices: none -> 51.5 us  [the longest x8 29 us: gather_around(): lower.append(lax.ppermute(lower[-1] if lower else array, axis, pairs))]
    all_gather x1, waiting for transfers between devices: 51.3 us -> 0.01 us  [body(): lax.all_gather(down_weight, 'dp', axis=1, tiled=True)]
    ppermute x0 -> x15, starting transfers between devices: none -> 32.2 us  [the longest x7 32.1 us: gather_around(): upper.append(lax.ppermute(upper[-1] if upper else array, axis, back))]
    all_gather x4, waiting for transfers between devices: 66 us -> 43.6 us  [tensor_total(): return lax.all_gather(summed_half, 'tensor', axis=1, tiled=True)]
    all_gather x1, waiting for transfers between devices: 50.8 us -> 33.5 us  [body(): lax.all_gather(shards[4], 'dp', axis=0, tiled=True)]
    unnamed x295 -> x324, local copies, waits for them, and re-layouts: 17.8 us -> 34.2 us
  transfers between devices with their start and end apart: 18 -> 33, of which waited for: 16 -> 26; matrix products, arithmetic and copies ran while one was open for 13% -> 15% of each run, Pallas kernels for 0% -> 0%
where the time goes in v1:
time: 1350 us; the launch traced here: 1340 us
  waiting for transfers between devices  822 us (61%)
  local copies, waits for them, and re-layouts  146 us (11%)
  matrix products  125 us (9%)
  blocking collectives  104 us (8%)
  other arithmetic  94.5 us (7%)
  starting transfers between devices  33.4 us (2%)
  between operations  17.5 us (1%)
    unnamed x24, waiting for transfers between devices  324 us
    reduce_scatter x1, waiting for transfers between devices, body(): lax.psum_scatter(local_down_grad, 'dp', scatter_dimension=1, tiled=True)  125 us
    reduce_scatter x1, waiting for transfers between devices, body(): lax.psum_scatter(local_up_grad, 'dp', scatter_dimension=0, tiled=True)  124 us
    unnamed x1, blocking collectives  67.1 us
    all_gather x1, waiting for transfers between devices, body(): lax.all_gather(ada_weight, 'dp', axis=0, tiled=True)  63.9 us
    all_gather x4, waiting for transfers between devices, tensor_total(): return lax.all_gather(summed_half, 'tensor', axis=1, tiled=True)  43.6 us
    unnamed x324, local copies, waits for them, and re-layouts  34.2 us
    all_gather x1, waiting for transfers between devices, body(): lax.all_gather(shards[4], 'dp', axis=0, tiled=True)  33.5 us
  transfers between devices with their start and end apart: 33, of which 26 were waited for; matrix products, arithmetic and copies ran while one was open for 15% of the time, Pallas kernels for 0%

profile of v1, /device:TPU:0, one launch (start us, length us, event | category | flops | bytes accessed | tf_op | source)
XLA Modules:
  0.0 1342.8 jit_solution(14442718153704420574)
XLA Ops:
  13.1 23.5 %all-gather = bf16[16,72,8]{1,2,0:T(8,128)(2,1)S(1)} all-gather(bf16[1,72,8]{1,2,0:T(8,128)(2,1)S(1)} %bitcast.237), channel_id=1, replica_groups=mesh['dp'=16,'tensor'=2] {'dp'}, dimensions={0}, use_global_device_ids=true | all-gather | bytes 19584 | tf_op jit(solution)/shard_map/all_gather | solution.py:173
  44.7 28.4 %all-gather.13.cloned.1.call-done = bf16[1152,4,576]{2,0,1:T(8,128)(2,1)} async-done(((bf16[72,4,576]{2,0,1:T(8,128)(2,1)}), bf16[1152,4,576]{2,0,1:T(8,128)(2,1)}) %all-gather.13.cloned.1.call-update) | async-done | bytes 5308432 | tf_op jit(solution)/shard_map/all_gather | solution.py:172
  73.1 8.5 copy.425
  81.6 63.9 %all-gather.11.cloned.1.call-done = bf16[1152,3456]{1,0:T(8,128)(2,1)} async-done(((bf16[72,3456]{1,0:T(8,128)(2,1)}), bf16[1152,3456]{1,0:T(8,128)(2,1)}) %all-gather.11.cloned.1.call-update) | async-done | bytes 7962640 | tf_op jit(solution)/shard_map/all_gather | solution.py:171
  240.0 20.6 %reduce-scatter.29.cloned.1.call-done = f32[576,256]{1,0:T(8,128)} async-done(((f32[1152,256]{1,0:T(8,128)}), f32[576,256]{1,0:T(8,128)}) %reduce-scatter.29.cloned.1.call-update) | async-done | bytes 589840
  261.4 9.2 collective-permute-done
  319.8 10.3 collective-permute-done.12
  378.8 7.3 fusion.21
  386.1 33.5 %all-gather.23.cloned.1.call-done = bf16[1152,2304]{1,0:T(8,128)(2,1)} async-done(((bf16[72,2304]{1,0:T(8,128)(2,1)}), bf16[1152,2304]{1,0:T(8,128)(2,1)}) %all-gather.23.cloned.1.call-update) | async-done | bytes 5308432 | tf_op jit(solution)/shard_map/all_gather | solution.py:229
  431.1 14.6 %reduce-scatter.33.cloned.1.call-done = f32[576,256]{1,0:T(8,128)} async-done(((f32[1152,256]{1,0:T(8,128)}), f32[576,256]{1,0:T(8,128)}) %reduce-scatter.33.cloned.1.call-update) | async-done | bytes 589840
  445.7 24.0 %reduce-scatter.31.cloned.1.call-done = f32[576,256]{1,0:T(8,128)} async-done(((f32[1152,256]{1,0:T(8,128)}), f32[576,256]{1,0:T(8,128)}) %reduce-scatter.31.cloned.1.call-update) | async-done | bytes 589840
  470.1 23.9 %all-gather.25.cloned.1.call-done = f32[256,1152]{0,1:T(8,128)} async-done(((f32[256,576]{0,1:T(8,128)}), f32[256,1152]{0,1:T(8,128)}) %all-gather.25.cloned.1.call-update) | async-done | bytes 1179664 | tf_op jit(solution)/shard_map/all_gather | solution.py:88
  498.6 19.7 %all-gather.21.cloned.1.call-done = f32[256,1152]{0,1:T(8,128)} async-done(((f32[256,576]{0,1:T(8,128)}), f32[256,1152]{0,1:T(8,128)}) %all-gather.21.cloned.1.call-update) | async-done | bytes 1179664 | tf_op jit(solution)/shard_map/all_gather | solution.py:88
  606.4 10.4 while.35
  662.4 21.9 %reduce-scatter.35.cloned.1.call-done = f32[576,256]{1,0:T(8,128)} async-done(((f32[1152,256]{1,0:T(8,128)}), f32[576,256]{1,0:T(8,128)}) %reduce-scatter.35.cloned.1.call-update) | async-done | bytes 589840
  702.2 7.6 fusion.139
  718.9 10.0 fusion.135
  733.8 67.1 %all-reduce.13 = (f32[1152,8]{0,1:T(8,128)S(1)}, f32[8]{0:T(128)}, f32[9,576]{1,0:T(8,128)}) all-reduce(f32[1152,8]{0,1:T(8,128)S(1)} %fusion.120, f32[8]{0:T(128)S(1)} %neg.58, f32[9,576]{1,0:T(8,128)S(1)} %pad_add_fusion), channel_id=8, replica_groups=mesh['dp'=16,'tensor'=2] {'dp'}, use_global_device_ids=true, to_apply=%region_43.45.clone | all-reduce | flops 14408 | bytes 115264
  807.0 7.9 psum.21
  815.5 28.3 %reduce-scatter.23.cloned.1.call-done = f32[72,4,576]{2,0,1:T(8,128)} async-done(((f32[1152,4,576]{2,0,1:T(8,128)}), f32[72,4,576]{2,0,1:T(8,128)}) %reduce-scatter.23.cloned.1.call-update) | async-done | bytes 663568 | tf_op jit(solution)/shard_map/reduce_scatter | solution.py:298
  846.0 65.6 %reduce-scatter.39.cloned.1.call-done = f32[576,72]{0,1:T(8,128)} async-done(((f32[576,1152]{0,1:T(8,128)}), f32[576,72]{0,1:T(8,128)}) %reduce-scatter.39.cloned.1.call-update) | async-done | bytes 165904
  911.6 124.2 %reduce-scatter.25.cloned.1.call-done = f32[72,2304]{1,0:T(8,128)} async-done(((f32[1152,2304]{1,0:T(8,128)}), f32[72,2304]{1,0:T(8,128)}) %reduce-scatter.25.cloned.1.call-update) | async-done | bytes 663568 | tf_op jit(solution)/shard_map/reduce_scatter | solution.py:301
  1035.9 124.8 %reduce-scatter.27.cloned.1.call-done = f32[2304,72]{0,1:T(8,128)} async-done(((f32[2304,1152]{0,1:T(8,128)}), f32[2304,72]{0,1:T(8,128)}) %reduce-scatter.27.cloned.1.call-update) | async-done | bytes 663568 | tf_op jit(solution)/shard_map/reduce_scatter | solution.py:302
  1160.7 174.8 %reduce-scatter.37.cloned.1.call-done = f32[72,3456]{1,0:T(8,128)} async-done(((f32[1152,3456]{1,0:T(8,128)}), f32[72,3456]{1,0:T(8,128)}) %reduce-scatter.37.cloned.1.call-update) | async-done | bytes 995344
  (619 shorter events, 412.0 us)
Async XLA Ops:
  7.2 65.9 %all-gather.13.cloned.1.call-start = ((), (), s32[]{:S(2)}) async-start(), calls=%async_computation.10 | async-start | bytes 6266880 | tf_op jit(solution)/shard_map/all_gather | solution.py:172
  9.1 136.4 %all-gather.11.cloned.1.call-start = ((), (), s32[]{:S(2)}) async-start(), calls=%async_computation.9 | async-start | bytes 8460288 | tf_op jit(solution)/shard_map/all_gather | solution.py:171
  9.9 227.0 %all-gather.15.cloned.1.call-start = ((), (), s32[]{:S(2)}) async-start(), calls=%async_computation.11 | async-start | bytes 1566720 | tf_op jit(solution)/shard_map/all_gather | solution.py:174
  10.6 250.0 %reduce-scatter.29.cloned.1.call-start = ((), (), s32[]{:S(2)}) async-start(), calls=%async_computation.21 | async-start | bytes 1769472
  240.0 127.9 %all-gather.17.cloned.1.call-start = ((), (), s32[]{:S(2)}) async-start(), calls=%async_computation.12 | async-start | bytes 1769472 | tf_op jit(solution)/shard_map/all_gather | solution.py:88
  260.7 118.1 %all-gather.19.cloned.1.call-start = ((), (), s32[]{:S(2)}) async-start(), calls=%async_computation.13 | async-start | bytes 5640192 | tf_op jit(solution)/shard_map/all_gather | solution.py:176
  261.2 158.3 %all-gather.23.cloned.1.call-start = ((), (), s32[]{:S(2)}) async-start(), calls=%async_computation.15 | async-start | bytes 5640192 | tf_op jit(solution)/shard_map/all_gather | solution.py:229
  289.2 14.5 %collective-permute-start.10 = (bf16[72,2304]{1,0:T(8,128)(2,1)S(1)}, bf16[72,2304]{1,0:T(8,128)(2,1)S(1)}, u32[]{:S(2)}, u32[]{:S(2)}) collective-permute-start(bf16[72,2304]{1,0:T(8,128)(2,1)S(1)} %collective-permute-done.9), channel_id=1, source_target_pairs={{2,0},{4,2},{6,4},{8,6},{10,8},{12,10},{14,12},{16,14},{18,16},{20... | collective-permute-start | bytes 995336 | tf_op jit(solution)/shard_map/ppermute | solution.py:29
  298.5 12.0 collective-permute-start.4
  314.0 16.2 %collective-permute-start.12 = (bf16[72,2304]{1,0:T(8,128)(2,1)S(1)}, bf16[72,2304]{1,0:T(8,128)(2,1)}, u32[]{:S(2)}, u32[]{:S(2)}) collective-permute-start(bf16[72,2304]{1,0:T(8,128)(2,1)S(1)} %collective-permute-done.11), channel_id=1, source_target_pairs={{2,0},{4,2},{6,4},{8,6},{10,8},{12,10},{14,12},{16,14},{18,16},{20... | collective-permute-start | bytes 995336 | tf_op jit(solution)/shard_map/ppermute | solution.py:29
  319.8 16.5 %collective-permute-start.6 = (bf16[72,2304]{1,0:T(8,128)(2,1)S(1)}, bf16[72,2304]{1,0:T(8,128)(2,1)}, u32[]{:S(2)}, u32[]{:S(2)}) collective-permute-start(bf16[72,2304]{1,0:T(8,128)(2,1)S(1)} %collective-permute-done.5), channel_id=1, source_target_pairs={{0,2},{2,4},{4,6},{6,8},{8,10},{10,12},{12,14},{14,16},{16,18},{18... | collective-permute-start | bytes 995336 | tf_op jit(solution)/shard_map/ppermute | solution.py:27
  330.1 10.6 collective-permute-start.13
  336.3 109.4 %reduce-scatter.33.cloned.1.call-start = ((), (), s32[]{:S(2)}) async-start(), calls=%async_computation.23 | async-start | bytes 1769472
  340.7 20.6 %collective-permute-start.14 = (bf16[72,2304]{1,0:T(8,128)(2,1)}, bf16[72,2304]{1,0:T(8,128)(2,1)S(1)}, u32[]{:S(2)}, u32[]{:S(2)}) collective-permute-start(bf16[72,2304]{1,0:T(8,128)(2,1)} %collective-permute-done.13), channel_id=1, source_target_pairs={{2,0},{4,2},{6,4},{8,6},{10,8},{12,10},{14,12},{16,14},{18,16},{20... | collective-permute-start | bytes 995336 | tf_op jit(solution)/shard_map/ppermute | solution.py:29
  425.1 44.7 %reduce-scatter.31.cloned.1.call-start = ((), (), s32[]{:S(2)}) async-start(), calls=%async_computation.22 | async-start | bytes 1769472
  431.1 62.9 %all-gather.25.cloned.1.call-start = ((), (), s32[]{:S(2)}) async-start(), calls=%async_computation.16 | async-start | bytes 1769472 | tf_op jit(solution)/shard_map/all_gather | solution.py:88
  445.7 72.6 %all-gather.21.cloned.1.call-start = ((), (), s32[]{:S(2)}) async-start(), calls=%async_computation.14 | async-start | bytes 1769472 | tf_op jit(solution)/shard_map/all_gather | solution.py:88
  469.8 214.6 %reduce-scatter.35.cloned.1.call-start = ((), (), s32[]{:S(2)}) async-start(), calls=%async_computation.24 | async-start | bytes 1769472
  662.4 47.5 %all-gather.27.cloned.1.call-start = ((), (), s32[]{:S(2)}) async-start(), calls=%async_computation.17 | async-start | bytes 1769472 | tf_op jit(solution)/shard_map/all_gather | solution.py:88
  684.4 159.5 %reduce-scatter.23.cloned.1.call-start = ((), (), s32[]{:S(2)}) async-start(), calls=%async_computation.18 | async-start | bytes 12533760 | tf_op jit(solution)/shard_map/reduce_scatter | solution.py:298
  690.6 221.0 %reduce-scatter.39.cloned.1.call-start = ((), (), s32[]{:S(2)}) async-start(), calls=%async_computation.26 | async-start | bytes 3133440
  694.1 341.8 %reduce-scatter.25.cloned.1.call-start = ((), (), s32[]{:S(2)}) async-start(), calls=%async_computation.19 | async-start | bytes 11280384 | tf_op jit(solution)/shard_map/reduce_scatter | solution.py:301
  701.1 459.6 %reduce-scatter.27.cloned.1.call-start = ((), (), s32[]{:S(2)}) async-start(), calls=%async_computation.20 | async-start | bytes 11280384 | tf_op jit(solution)/shard_map/reduce_scatter | solution.py:302
  709.8 625.7 %reduce-scatter.37.cloned.1.call-start = ((), (), s32[]{:S(2)}) async-start(), calls=%async_computation.25 | async-start | bytes 16920576
  (161 other events, 1872.4 us)
Sparse Core Ops, SparseCore 0:
  10.8 62.2 all-gather.12
  75.3 70.2 all-gather.10
  147.7 37.7 all-gather.14
  240.1 20.4 reduce-scatter.28
  262.0 22.7 all-gather.16
  286.9 70.7 all-gather.18
  359.9 59.6 all-gather.22
  425.2 20.4 reduce-scatter.32
  447.9 21.8 reduce-scatter.30
  471.2 22.7 all-gather.24
  495.5 22.7 all-gather.20
  662.5 21.8 reduce-scatter.34
  685.9 22.7 all-gather.26
  712.7 131.1 reduce-scatter.22
  848.2 63.4 reduce-scatter.38
  916.1 119.7 reduce-scatter.24
  1040.3 120.2 reduce-scatter.26
  1165.2 170.2 reduce-scatter.36
